TPU v7x, 128 devices: a whole 4x4x4 slice. The times are simulated.
128 devices in a mesh: dp: 128 (over x, z, y, core).
Axes of the slice: x: 4, y: 4, z: 4, core: 2. Of those that a mesh axis runs over, the one named last changes fastest.
Arguments:
- token_ids: int32 [131072], P('dp'), may hold values from 0 to 31999, as said below
- tokens: bfloat16 [131072, 4096], P('dp'), may hold values from -64 to 64
- frozen_weight: bfloat16 [4096, 1024], replicated, may hold values from -0.09375 to 0.09375
- adapter_down: bfloat16 [4096, 128], replicated, may hold values from -0.09375 to 0.09375
- adapter_up: bfloat16 [128, 1024], replicated, may hold values from -1.5 to 1.5
- gate_weight: bfloat16 [4096, 8], replicated, may hold values from -1 to 1
- upstream: bfloat16 [131072, 1024], P('dp'), may hold values from -6 to 6
Outputs:
- projected: bfloat16 [131072, 1024], P('dp')
- input_grad: bfloat16 [131072, 4096], P('dp')
- clipped_down: float32 [4096, 128], replicated
- clipped_up: float32 [128, 1024], replicated
- clipped_gate: float32 [4096, 8], replicated
- load: float32 [8], replicated
- entropy: float32 [], replicated
Inputs may be any that keep to these rules, and one draw needn't show every extreme that they name: `token_ids`: within each device's block of 1024 tokens the live tokens (id not 0) come first, 256 or more of them, and padding (id 0) fills the rest; the last block is wholly live.
All inputs are finite; a program needn't handle non-finite values.
Results may differ from a plain program's by a relative error of at most 0.0095.
Values sent between devices are 32-bit elements; how exact they have to be, the bound alone decides.
A program may use at most 192 MiB of HBM per device.

v0:
```python
import math
import jax
import jax.numpy as jnp
from jax import lax
from jax.sharding import Mesh
from jax.sharding import PartitionSpec as P

DP = ("dp_0", "dp_1", "dp_2", "dp_3")


def over_axes(x, axes):
    for axis in axes:
        x = lax.psum(x, axis)
    return x


def left_dot(first, second):
    return lax.dot_general(
        first, second, (((0,), (0,)), ((), ())), preferred_element_type=jnp.float32
    )


def right_dot(first, second):
    return lax.dot_general(
        first, second, (((1,), (1,)), ((), ())), preferred_element_type=jnp.float32
    )


def exact_left(tokens, matrix):
    upper = matrix.astype(jnp.bfloat16)
    lower = (matrix - upper.astype(jnp.float32)).astype(jnp.bfloat16)
    return left_dot(tokens, upper) + left_dot(tokens, lower)


def share_stats(local):
    return (over_axes(local[0], DP), over_axes(local[1], DP), over_axes(local[2], DP))


def reduce_clip(terms, finish, limit):
    summed = lax.psum((terms[0], terms[1], terms[2]), DP)
    grads = finish(summed)
    total = (
        jnp.sum(grads[0] * grads[0]) + jnp.sum(grads[1] * grads[1]) + jnp.sum(grads[2] * grads[2])
    )
    factor = jnp.minimum(1.0, limit / jnp.sqrt(total))
    return (grads[0] * factor, grads[1] * factor, grads[2] * factor)


def on_device(token_ids, tokens, frozen_weight, adapter_down, adapter_up, gate_weight, upstream):
    width = tokens.shape[1]
    experts = gate_weight.shape[1]
    ranks = adapter_down.shape[1]
    rank = ranks // experts
    outputs = frozen_weight.shape[1]
    rows = tokens.shape[0]
    live = (token_ids != 0).astype(jnp.float32)
    base = jnp.dot(tokens, frozen_weight, preferred_element_type=jnp.float32)
    logits = jnp.dot(tokens, gate_weight, preferred_element_type=jnp.float32)
    prob = jax.nn.softmax(logits, axis=1)
    logp = jax.nn.log_softmax(logits, axis=1)
    low = jnp.dot(tokens, adapter_down, preferred_element_type=jnp.float32).astype(jnp.bfloat16)
    spread = jnp.repeat(prob, rank, axis=1)
    weighted = (low.astype(jnp.float32) * spread).astype(jnp.bfloat16)
    projected = (
        base + 2.0 * jnp.dot(weighted, adapter_up, preferred_element_type=jnp.float32)
    ).astype(jnp.bfloat16)
    masked = upstream * live.astype(jnp.bfloat16)[:, None]
    grad_up = 2.0 * left_dot(weighted, masked)
    back = right_dot(masked, adapter_up)
    gate_task = 2.0 * jnp.sum((low.astype(jnp.float32) * back).reshape(rows, experts, rank), axis=2)
    low_grad = (2.0 * spread * back).astype(jnp.bfloat16)
    grad_down = left_dot(tokens, low_grad)
    ent_tok = -jnp.sum(prob * logp, axis=1)
    local_stats = (jnp.sum(live[:, None] * prob, axis=0), jnp.sum(live * ent_tok), jnp.sum(live))

    def jac(vector):
        return prob * (vector - jnp.sum(prob * vector, axis=1, keepdims=True))

    plain_z = jac(gate_task) + 50.0 * live[:, None] * prob * (logp + ent_tok[:, None])
    frozen_back = right_dot(masked, frozen_weight) + right_dot(low_grad, adapter_down)
    count = width * ranks + ranks * outputs + width * experts
    limit = math.sqrt(count)
    load_all, ent_all, live_all = share_stats(local_stats)
    gate_z = plain_z + 2.0 * experts * 100.0 / live_all * live[:, None] * jac(load_all[None, :])
    terms = (grad_down, grad_up, exact_left(tokens, gate_z))

    def finish(summed):
        return summed

    clipped = reduce_clip(terms, finish, limit)
    input_grad = frozen_back + jnp.dot(
        gate_z, gate_weight.astype(jnp.float32).T, precision=lax.Precision.HIGHEST
    )
    return (
        projected,
        input_grad.astype(jnp.bfloat16),
        clipped[0],
        clipped[1],
        clipped[2],
        load_all / live_all,
        ent_all / live_all,
    )


def solution(mesh):
    torus = Mesh(mesh.devices.reshape(4, 4, 4, 2), ("dp_0", "dp_1", "dp_2", "dp_3"))
    return jax.shard_map(
        on_device,
        mesh=torus,
        in_specs=(P(DP), P(DP, None), P(), P(), P(), P(), P(DP, None)),
        out_specs=(P(DP, None), P(DP, None), P(), P(), P(), P(), P()),
        check_vma=False,
    )
```

profile of v0, /device:TPU:1, one launch (start us, length us, event | category | flops | bytes accessed | tf_op | source)
XLA Modules:
  0.0 243.0 jit_solution(7929073517609321213)
XLA Ops:
  7.2 0.0 copy-start
  7.2 0.0 all-reduce.7.cloned.1.call-start
  7.2 0.0 copy-start.1
  7.2 5.8 %fusion.21 = (f32[1024]{0:T(1024)S(1)}, f32[1024,8]{0,1:T(8,128)S(1)}) fusion(bf16[1024,4096]{1,0:T(8,128)(2,1)} %param.8, bf16[4096,8]{0,1:T(8,128)(2,1)} %param.12), kind=kOutput, calls=%fused_computation.48 | convolution fusion | flops 67116032 | bytes 8491008 | tf_op jit(solution)/shard_map/dot_general | solution.py:58
  13.1 0.0 copy-start.8
  13.1 0.0 copy-start.2
  13.1 0.0 copy-start.3
  13.2 0.0 copy-done
  13.2 0.1 copy-done.1
  13.3 2.9 %fusion.10 = f32[1024,128]{0,1:T(8,128)S(1)} fusion(bf16[1024,4096]{1,0:T(8,128)(2,1)S(1)} %copy-done.1, bf16[4096,128]{1,0:T(8,128)(2,1)S(1)} %copy-done), kind=kOutput, calls=%fused_computation.14 | convolution fusion | flops 1074003968 | bytes 9961472 | tf_op jit(solution)/shard_map/dot_general | solution.py:61
  16.2 0.0 copy-done.8
  16.2 0.0 copy-done.2
  16.3 0.0 copy-done.3
  16.3 1.5 fusion.16
  17.8 0.1 bitcast_reduce_fusion
  17.9 0.1 multiply_reduce_fusion.6
  18.0 0.6 select_reduce_fusion
  18.6 9.9 %all-reduce.3 = (f32[8]{0:T(128)S(1)}, f32[]{:T(128)}, f32[]{:T(128)}) all-reduce(f32[8]{0:T(128)S(1)} %get-tuple-element.16, f32[]{:T(128)} %get-tuple-element.18, f32[]{:T(128)} %get-tuple-element.17), channel_id=1, replica_groups=mesh['dp_0'=4,'dp_1'=4,'dp_2'=4,'dp_3'=2] {'dp_0'}, use_global_device_ids=true, to_apply=%region_11.12 | all-reduce | flops 10 | bytes 80 | tf_op jit(solution)/shard_map/psum | solution.py:13
  28.5 10.4 %all-reduce.2 = (f32[8]{0:T(128)S(1)}, f32[]{:T(128)}, f32[]{:T(128)}) all-reduce(f32[8]{0:T(128)S(1)} %get-tuple-element.28, f32[]{:T(128)} %get-tuple-element.29, f32[]{:T(128)} %get-tuple-element.30), channel_id=1, replica_groups=mesh['dp_0'=4,'dp_1'=4,'dp_2'=4,'dp_3'=2] {'dp_1'}, use_global_device_ids=true, to_apply=%region_12.13 | all-reduce | flops 10 | bytes 80 | tf_op jit(solution)/shard_map/psum | solution.py:13
  38.9 9.3 %all-reduce.1 = (f32[8]{0:T(128)S(1)}, f32[]{:T(128)}, f32[]{:T(128)}) all-reduce(f32[8]{0:T(128)S(1)} %get-tuple-element.25, f32[]{:T(128)} %get-tuple-element.26, f32[]{:T(128)} %get-tuple-element.27), channel_id=1, replica_groups=mesh['dp_0'=4,'dp_1'=4,'dp_2'=4,'dp_3'=2] {'dp_2'}, use_global_device_ids=true, to_apply=%region_13.14 | all-reduce | flops 10 | bytes 80 | tf_op jit(solution)/shard_map/psum | solution.py:13
  48.2 9.5 %all-reduce.4 = (f32[8]{0:T(128)S(1)}, f32[]{:T(128)}, f32[]{:T(128)}) all-reduce(f32[8]{0:T(128)S(1)} %get-tuple-element.22, f32[]{:T(128)} %get-tuple-element.23, f32[]{:T(128)} %get-tuple-element.24), channel_id=1, replica_groups=mesh['dp_0'=4,'dp_1'=4,'dp_2'=4,'dp_3'=2] {'dp_3'}, use_global_device_ids=true, to_apply=%region_14.15 | all-reduce | flops 10 | bytes 80 | tf_op jit(solution)/shard_map/psum | solution.py:13
  57.7 0.1 multiply_reduce_fusion.3
  58.4 0.0 copy-start.5
  58.5 6.0 %convolution_bitcast_fusion = f32[4096,128]{0,1:T(8,128)} fusion(bf16[1024,128]{0,1:T(8,128)(2,1)S(1)} %get-tuple-element.36, bf16[1024,4096]{1,0:T(8,128)(2,1)} %param.8), kind=kOutput, calls=%fused_computation.1 | convolution fusion | flops 1073741824 | bytes 10747904 | tf_op jit(solution)/shard_map/dot_general | solution.py:18
  64.5 0.0 copy-done.5
  64.5 1.3 fusion.7
  65.8 0.1 multiply_add_fusion
  65.9 4.7 %fusion.18 = f32[8,4096]{1,0:T(8,128)S(1)} fusion(bf16[1024,4096]{1,0:T(8,128)(2,1)} %param.8, f32[1024,8]{0,1:T(8,128)S(1)} %multiply_add_fusion), kind=kOutput, calls=%fused_computation.38 | convolution fusion | flops 67117056 | bytes 8552448 | tf_op jit(solution)/shard_map/dot_general | solution.py:18
  70.6 0.1 slice-done.1
  70.7 1.9 fusion
  72.6 0.0 all-reduce.7.cloned.1.call-update
  72.6 10.4 %fusion.23 = f32[1024,4096]{1,0:T(8,128)} fusion(f32[1024,8]{0,1:T(8,128)S(1)} %multiply_add_fusion, bf16[4096,8]{0,1:T(8,128)(2,1)S(1)} %copy-done.7), kind=kOutput, calls=%fused_computation.50 | convolution fusion | flops 402653184 | bytes 16875520 | tf_op jit(solution)/shard_map/dot_general | solution.py:91
  83.0 12.7 %fusion.22 = f32[1024,1024]{1,0:T(8,128)S(1)} fusion(bf16[1024,4096]{1,0:T(8,128)(2,1)} %param.8, bf16[4096,1024]{1,0:T(8,128)(2,1)} %param.9), kind=kOutput, calls=%fused_computation.49 | convolution fusion | flops 8589934592 | bytes 20971520 | tf_op jit(solution)/shard_map/dot_general | solution.py:57
  95.7 0.0 copy-start.4
  95.7 0.0 copy-start.6
  95.8 14.6 %fusion.5 = f32[1024,4096]{1,0:T(8,128)} fusion(bf16[4096,1024]{1,0:T(8,128)(2,1)} %param.9, bf16[1024,1024]{1,0:T(8,128)(2,1)S(1)} %copy-done.2, bf16[1024]{0:T(1024)(128)(2,1)S(1)} %get-tuple-element.41), kind=kOutput, calls=%fused_computation.10 | convolution fusion | flops 8590983168 | bytes 27265024 | tf_op jit(solution)/shard_map/dot_general | solution.py:24
  110.3 1.2 broadcast_divide_fusion
  111.5 0.0 copy-done.4
  111.5 2.1 add_convert_fusion.1
  114.9 15.4 %add_convert_fusion = bf16[1024,4096]{1,0:T(8,128)(2,1)} fusion(f32[1024,4096]{1,0:T(8,128)} %fusion.23, f32[1024,4096]{1,0:T(8,128)} %fusion.5, bf16[1024,128]{0,1:T(8,128)(2,1)S(1)} %get-tuple-element.36, bf16[4096,128]{1,0:T(8,128)(2,1)S(1)} %copy-done), kind=kOutput, calls=%fused_computation | convolution fusion | flops 1086324736 | bytes 43253760 | tf_op jit(solution)/shard_map/dot_general | solution.py:24
  130.3 89.6 %all-reduce.7.cloned.1.call-done = (f32[4096,128]{0,1:T(8,128)}, f32[128,1024]{1,0:T(8,128)}, f32[4096,8]{0,1:T(8,128)}) async-done(((f32[4096,128]{0,1:T(8,128)}, f32[128,1024]{1,0:T(8,128)}, f32[4096,8]{0,1:T(8,128)}), (f32[4096,128]{0,1:T(8,128)}, f32[128,1024]{1,0:T(8,128)}, f32[4096,8]{0,1:T(8,128)})) %all-reduce.7.cloned.1.call-update) | async-done | bytes 2752528 | tf_op jit(solution)/shard_map/psum | solution.py:40
  219.9 2.7 %multiply_reduce_fusion = f32[]{:T(128)} fusion(f32[4096,128]{0,1:T(8,128)} %get-tuple-element.19), kind=kLoop, calls=%fused_computation.5 | loop fusion | flops 1048575 | bytes 2097156 | tf_op jit(solution)/shard_map/reduce_sum | solution.py:43
  222.6 1.8 multiply_reduce_fusion.1
  224.4 1.5 multiply_reduce_fusion.2
  227.9 1.8 broadcast_multiply_fusion
  229.7 1.9 broadcast_multiply_fusion.1
  231.6 1.6 broadcast_multiply_fusion.2
  233.2 1.8 copy.14
  (13 shorter events, 0.1 us)
Async XLA Ops:
  7.2 6.0 %copy-start = (bf16[4096,128]{1,0:T(8,128)(2,1)S(1)}, bf16[4096,128]{1,0:T(8,128)(2,1)}, u32[]{:S(2)}) copy-start(bf16[4096,128]{1,0:T(8,128)(2,1)} %param.10) | copy-start | bytes 3145732
  7.2 212.7 %all-reduce.7.cloned.1.call-start = ((), (), s32[]{:S(2)}) async-start(), calls=%async_computation | async-start | bytes 5505024 | tf_op jit(solution)/shard_map/psum | solution.py:40
  7.2 6.1 %copy-start.1 = (bf16[1024,4096]{1,0:T(8,128)(2,1)S(1)}, bf16[1024,4096]{1,0:T(8,128)(2,1)}, u32[]{:S(2)}) copy-start(bf16[1024,4096]{1,0:T(8,128)(2,1)} %param.8) | copy-start | bytes 25165828
  13.1 3.2 %copy-start.8 = (s32[1024]{0:T(1024)S(1)}, s32[1024]{0:T(1024)}, u32[]{:S(2)}) copy-start(s32[1024]{0:T(1024)} %param.7) | copy-start | bytes 12292
  13.1 3.2 %copy-start.2 = (bf16[1024,1024]{1,0:T(8,128)(2,1)S(1)}, bf16[1024,1024]{1,0:T(8,128)(2,1)}, u32[]{:S(2)}) copy-start(bf16[1024,1024]{1,0:T(8,128)(2,1)} %param.13) | copy-start | bytes 6291460
  13.1 3.2 %copy-start.3 = (bf16[128,1024]{1,0:T(8,128)(2,1)S(1)}, bf16[128,1024]{1,0:T(8,128)(2,1)}, u32[]{:S(2)}) copy-start(bf16[128,1024]{1,0:T(8,128)(2,1)} %param.11) | copy-start | bytes 786436
  58.4 6.0 %copy-start.5 = (bf16[1024,128]{0,1:T(8,128)(2,1)S(1)}, bf16[1024,128]{0,1:T(8,128)(2,1)}, u32[]{:S(2)}) copy-start(bf16[1024,128]{0,1:T(8,128)(2,1)} %get-tuple-element.38) | copy-start | bytes 786436
  64.5 6.1 %slice-start = ((s8[8388608]{0:T(1024)(128)(4,1)}), s8[4194304]{0:T(1024)(128)(4,1)S(1)}, s32[]{:S(2)}) async-start(s8[8388608]{0:T(1024)(128)(4,1)} %bitcast.34), calls=%async_computation.1 | async-start | bytes 8388608
  65.9 4.9 %slice-start.1 = ((s8[8388608]{0:T(1024)(128)(4,1)}), s8[4194304]{0:T(1024)(128)(4,1)S(1)}, s32[]{:S(2)}) async-start(s8[8388608]{0:T(1024)(128)(4,1)} %bitcast.34), calls=%async_computation.2 | async-start | bytes 8388608
  70.7 1.9 copy-start.7
  95.7 15.8 %copy-start.4 = (bf16[128,1024]{1,0:T(8,128)(2,1)S(1)}, bf16[128,1024]{1,0:T(8,128)(2,1)}, u32[]{:S(2)}) copy-start(bf16[128,1024]{1,0:T(8,128)(2,1)} %param.11) | copy-start | bytes 786436
  95.7 15.7 %copy-start.6 = (bf16[1024,128]{0,1:T(8,128)(2,1)S(1)}, bf16[1024,128]{0,1:T(8,128)(2,1)}, u32[]{:S(2)}) copy-start(bf16[1024,128]{0,1:T(8,128)(2,1)} %get-tuple-element.38) | copy-start | bytes 786436
Sparse Core Ops, SparseCore 0:
  72.7 147.1 all-reduce.6
where the time goes:
time: 243 us
  waiting for transfers between devices  89.6 us (37%)
  matrix products  79.3 us (33%)
  blocking collectives  39.1 us (16%)
  between operations  19.4 us (8%)
  other arithmetic  13.5 us (6%)
    psum x1, waiting for transfers between devices, reduce_clip(): summed = lax.psum((terms[0], terms[1], terms[2]), DP)  89.6 us
    psum x4, blocking collectives, over_axes(): x = lax.psum(x, axis)  39.1 us
    dot_general x3, matrix products, right_dot(): lax.dot_general(first, second, (((1,), (1,)), ((), ())), preferred_elemen...  31.5 us
    dot_general x4, matrix products, left_dot(): lax.dot_general(first, second, (((0,), (0,)), ((), ())), preferred_elemen...  13.9 us
    dot_general x1, matrix products, on_device(): base = jnp.dot(tokens, frozen_weight, preferred_element_type=jnp.float32)  12.7 us
    dot_general x1, matrix products, on_device(): jnp.dot(gate_z, gate_weight.astype(jnp.float32).T, precision=lax.Precisio...  10.4 us
    dot_general x1, matrix products, on_device(): logits = jnp.dot(tokens, gate_weight, preferred_element_type=jnp.float32)  5.81 us
    mul x3, other arithmetic, reduce_clip(): return (grads[0] * factor, grads[1] * factor, grads[2] * factor)  5.23 us
  transfers between devices with their start and end apart: 1, of which 1 were waited for; matrix products, arithmetic and copies ran while one was open for 23% of the time, Pallas kernels for 0%

commit v1 on v0

--- a/solution.py
+++ b/solution.py
@@ -10,7 +10,7 @@
 
 def over_axes(x, axes):
     for axis in axes:
-        x = lax.psum(x, axis)
+        x = jnp.sum(lax.all_gather(x, axis), axis=0)
     return x
 
 

time: 243 us -> 263 us (1.082)
  local copies, waits for them, and re-layouts: 2.14 us -> 17.5 us
  other arithmetic: 13.5 us -> 18.4 us
    psum x4 -> x0, blocking collectives: 39.1 us -> none  [over_axes(): x = lax.psum(x, axis)]
    unnamed x0 -> x4, blocking collectives: none -> 36.5 us
    unnamed x23 -> x57, local copies, waits for them, and re-layouts: 2.14 us -> 17.2 us
    reduce_sum x0 -> x12, other arithmetic: none -> 4.88 us  [over_axes(): x = jnp.sum(lax.all_gather(x, axis), axis=0)]
  transfers between devices with their start and end apart: 1 -> 1, of which waited for: 1 -> 1; matrix products, arithmetic and copies ran while one was open for 23% -> 22% of each run, Pallas kernels for 0% -> 0%
where the time goes in v1:
time: 263 us
  waiting for transfers between devices  89 us (34%)
  matrix products  79.3 us (30%)
  blocking collectives  36.5 us (14%)
  between operations  22 us (8%)
  other arithmetic  18.4 us (7%)
  local copies, waits for them, and re-layouts  17.5 us (7%)
    psum x1, waiting for transfers between devices, reduce_clip(): summed = lax.psum((terms[0], terms[1], terms[2]), DP)  89 us
    unnamed x4, blocking collectives  36.5 us
    dot_general x3, matrix products, right_dot(): lax.dot_general(first, second, (((1,), (1,)), ((), ())), preferred_elemen...  31.5 us
    unnamed x57, local copies, waits for them, and re-layouts  17.2 us
    dot_general x4, matrix products, left_dot(): lax.dot_general(first, second, (((0,), (0,)), ((), ())), preferred_elemen...  13.9 us
    dot_general x1, matrix products, on_device(): base = jnp.dot(tokens, frozen_weight, preferred_element_type=jnp.float32)  12.7 us
    dot_general x1, matrix products, on_device(): jnp.dot(gate_z, gate_weight.astype(jnp.float32).T, precision=lax.Precisio...  10.4 us
    dot_general x1, matrix products, on_device(): logits = jnp.dot(tokens, gate_weight, preferred_element_type=jnp.float32)  5.81 us
  transfers between devices with their start and end apart: 1, of which 1 were waited for; matrix products, arithmetic and copies ran while one was open for 22% of the time, Pallas kernels for 0%

profile of v1, /device:TPU:1, one launch (start us, length us, event | category | flops | bytes accessed | tf_op | source)
XLA Modules:
  0.0 262.7 jit_solution(10274909654023047768)
XLA Ops:
  7.2 5.8 %fusion.21 = (f32[1024]{0:T(1024)S(1)}, f32[1024,8]{0,1:T(8,128)S(1)}) fusion(bf16[1024,4096]{1,0:T(8,128)(2,1)} %param.8, bf16[4096,8]{0,1:T(8,128)(2,1)} %param.12), kind=kOutput, calls=%fused_computation.48 | convolution fusion | flops 67116032 | bytes 8491008 | tf_op jit(solution)/shard_map/dot_general | solution.py:58
  13.3 2.9 %fusion.10 = f32[1024,128]{0,1:T(8,128)S(1)} fusion(bf16[1024,4096]{1,0:T(8,128)(2,1)S(1)} %copy-done.1, bf16[4096,128]{1,0:T(8,128)(2,1)S(1)} %copy-done), kind=kOutput, calls=%fused_computation.14 | convolution fusion | flops 1074003968 | bytes 9961472 | tf_op jit(solution)/shard_map/dot_general | solution.py:61
  16.3 1.5 fusion.16
  18.0 0.6 select_reduce_fusion
  18.6 1.2 dynamic-slice
  20.5 1.4 dynamic-update-slice
  21.9 1.4 dynamic-update-slice.8
  23.3 0.2 dynamic-update-slice.4
  23.5 9.3 %all-reduce.15 = (f32[32]{0:T(128)S(1)}, f32[4]{0:T(128)S(1)}, f32[4]{0:T(128)S(1)}) all-reduce(f32[32]{0:T(128)S(1)} %dynamic-update-slice.4, f32[4]{0:T(128)S(1)} %dynamic-update-slice, f32[4]{0:T(128)S(1)} %dynamic-update-slice.8), channel_id=2, replica_groups=mesh['dp_0'=4,'dp_1'=4,'dp_2'=4,'dp_3'=2] {'dp_0'}, use_global_device_ids=true, to_apply=%add.4 | all-reduce | flops 40 | bytes 320
  32.9 0.6 dynamic-slice.1
  34.1 0.6 reduce_sum.217
  34.7 0.6 reduce_sum.231
  35.3 1.4 dynamic-update-slice.1
  36.7 1.4 dynamic-update-slice.9
  38.1 0.2 dynamic-update-slice.5
  38.3 9.7 %all-reduce.14 = (f32[32]{0:T(128)S(1)}, f32[4]{0:T(128)S(1)}, f32[4]{0:T(128)S(1)}) all-reduce(f32[32]{0:T(128)S(1)} %dynamic-update-slice.5, f32[4]{0:T(128)S(1)} %dynamic-update-slice.1, f32[4]{0:T(128)S(1)} %dynamic-update-slice.9), channel_id=3, replica_groups=mesh['dp_0'=4,'dp_1'=4,'dp_2'=4,'dp_3'=2] {'dp_1'}, use_global_device_ids=true, to_apply=%add.5 | all-reduce | flops 40 | bytes 320
  48.1 0.6 dynamic-slice.2
  49.4 0.6 reduce_sum.218
  50.0 0.6 reduce_sum.232
  50.6 1.4 dynamic-update-slice.2
  52.0 1.4 dynamic-update-slice.10
  53.6 8.7 %all-reduce.13 = (f32[32]{0:T(128)S(1)}, f32[4]{0:T(128)S(1)}, f32[4]{0:T(128)S(1)}) all-reduce(f32[32]{0:T(128)S(1)} %dynamic-update-slice.6, f32[4]{0:T(128)S(1)} %dynamic-update-slice.2, f32[4]{0:T(128)S(1)} %dynamic-update-slice.10), channel_id=4, replica_groups=mesh['dp_0'=4,'dp_1'=4,'dp_2'=4,'dp_3'=2] {'dp_2'}, use_global_device_ids=true, to_apply=%add.6 | all-reduce | flops 40 | bytes 320
  62.4 0.6 dynamic-slice.3
  63.7 0.6 reduce_sum.219
  64.3 0.6 reduce_sum.233
  64.9 1.4 dynamic-update-slice.3
  66.3 1.4 dynamic-update-slice.11
  67.9 8.8 %all-reduce.16 = (f32[16]{0:T(128)S(1)}, f32[2]{0:T(128)S(1)}, f32[2]{0:T(128)S(1)}) all-reduce(f32[16]{0:T(128)S(1)} %dynamic-update-slice.7, f32[2]{0:T(128)S(1)} %dynamic-update-slice.3, f32[2]{0:T(128)S(1)} %dynamic-update-slice.11), channel_id=5, replica_groups=mesh['dp_0'=4,'dp_1'=4,'dp_2'=4,'dp_3'=2] {'dp_3'}, use_global_device_ids=true, to_apply=%add.7 | all-reduce | flops 20 | bytes 160
  76.9 0.6 reduce_sum.220
  78.2 6.0 %convolution_bitcast_fusion = f32[4096,128]{0,1:T(8,128)} fusion(bf16[1024,128]{0,1:T(8,128)(2,1)S(1)} %get-tuple-element.36, bf16[1024,4096]{1,0:T(8,128)(2,1)} %param.8), kind=kOutput, calls=%fused_computation.1 | convolution fusion | flops 1073741824 | bytes 10747904 | tf_op jit(solution)/shard_map/dot_general | solution.py:18
  84.2 1.3 fusion.7
  85.6 4.7 %fusion.18 = f32[8,4096]{1,0:T(8,128)S(1)} fusion(bf16[1024,4096]{1,0:T(8,128)(2,1)} %param.8, f32[1024,8]{0,1:T(8,128)S(1)} %multiply_add_fusion), kind=kOutput, calls=%fused_computation.38 | convolution fusion | flops 67117056 | bytes 8552448 | tf_op jit(solution)/shard_map/dot_general | solution.py:18
  90.5 1.9 fusion
  92.4 10.4 %fusion.23 = f32[1024,4096]{1,0:T(8,128)} fusion(f32[1024,8]{0,1:T(8,128)S(1)} %multiply_add_fusion, bf16[4096,8]{0,1:T(8,128)(2,1)S(1)} %copy-done.7), kind=kOutput, calls=%fused_computation.50 | convolution fusion | flops 402653184 | bytes 16875520 | tf_op jit(solution)/shard_map/dot_general | solution.py:91
  102.7 12.7 %fusion.22 = f32[1024,1024]{1,0:T(8,128)S(1)} fusion(bf16[1024,4096]{1,0:T(8,128)(2,1)} %param.8, bf16[4096,1024]{1,0:T(8,128)(2,1)} %param.9), kind=kOutput, calls=%fused_computation.49 | convolution fusion | flops 8589934592 | bytes 20971520 | tf_op jit(solution)/shard_map/dot_general | solution.py:57
  115.5 14.6 %fusion.5 = f32[1024,4096]{1,0:T(8,128)} fusion(bf16[4096,1024]{1,0:T(8,128)(2,1)} %param.9, bf16[1024,1024]{1,0:T(8,128)(2,1)S(1)} %copy-done.2, bf16[1024]{0:T(1024)(128)(2,1)S(1)} %get-tuple-element.41), kind=kOutput, calls=%fused_computation.10 | convolution fusion | flops 8590983168 | bytes 27265024 | tf_op jit(solution)/shard_map/dot_general | solution.py:24
  130.1 1.2 broadcast_divide_fusion
  131.2 2.1 add_convert_fusion.1
  133.3 0.6 reduce_sum.234
  135.2 15.4 %add_convert_fusion = bf16[1024,4096]{1,0:T(8,128)(2,1)} fusion(f32[1024,4096]{1,0:T(8,128)} %fusion.23, f32[1024,4096]{1,0:T(8,128)} %fusion.5, bf16[1024,128]{0,1:T(8,128)(2,1)S(1)} %get-tuple-element.36, bf16[4096,128]{1,0:T(8,128)(2,1)S(1)} %copy-done), kind=kOutput, calls=%fused_computation | convolution fusion | flops 1086324736 | bytes 43253760 | tf_op jit(solution)/shard_map/dot_general | solution.py:24
  150.7 89.0 %all-reduce.19.cloned.1.call-done = (f32[4096,128]{0,1:T(8,128)}, f32[128,1024]{1,0:T(8,128)}, f32[4096,8]{0,1:T(8,128)}) async-done(((f32[4096,128]{0,1:T(8,128)}, f32[128,1024]{1,0:T(8,128)}, f32[4096,8]{0,1:T(8,128)}), (f32[4096,128]{0,1:T(8,128)}, f32[128,1024]{1,0:T(8,128)}, f32[4096,8]{0,1:T(8,128)})) %all-reduce.19.cloned.1.call-update) | async-done | bytes 2752528 | tf_op jit(solution)/shard_map/psum | solution.py:40
  239.6 2.7 %multiply_reduce_fusion = f32[]{:T(128)} fusion(f32[4096,128]{0,1:T(8,128)} %get-tuple-element.19), kind=kLoop, calls=%fused_computation.5 | loop fusion | flops 1048575 | bytes 2097156 | tf_op jit(solution)/shard_map/reduce_sum | solution.py:43
  242.4 1.8 multiply_reduce_fusion.1
  244.2 1.5 multiply_reduce_fusion.2
  247.7 1.8 broadcast_multiply_fusion
  249.5 1.9 broadcast_multiply_fusion.1
  251.4 1.6 broadcast_multiply_fusion.2
  252.9 1.8 copy.14
  (63 shorter events, 1.7 us)
Async XLA Ops:
  7.2 6.0 %copy-start = (bf16[4096,128]{1,0:T(8,128)(2,1)S(1)}, bf16[4096,128]{1,0:T(8,128)(2,1)}, u32[]{:S(2)}) copy-start(bf16[4096,128]{1,0:T(8,128)(2,1)} %param.10) | copy-start | bytes 3145732
  7.2 232.5 %all-reduce.19.cloned.1.call-start = ((), (), s32[]{:S(2)}) async-start(), calls=%async_computation | async-start | bytes 5505024 | tf_op jit(solution)/shard_map/psum | solution.py:40
  7.2 6.1 %copy-start.1 = (bf16[1024,4096]{1,0:T(8,128)(2,1)S(1)}, bf16[1024,4096]{1,0:T(8,128)(2,1)}, u32[]{:S(2)}) copy-start(bf16[1024,4096]{1,0:T(8,128)(2,1)} %param.8) | copy-start | bytes 25165828
  13.1 3.2 %copy-start.8 = (s32[1024]{0:T(1024)S(1)}, s32[1024]{0:T(1024)}, u32[]{:S(2)}) copy-start(s32[1024]{0:T(1024)} %param.7) | copy-start | bytes 12292
  13.1 3.2 %copy-start.2 = (bf16[1024,1024]{1,0:T(8,128)(2,1)S(1)}, bf16[1024,1024]{1,0:T(8,128)(2,1)}, u32[]{:S(2)}) copy-start(bf16[1024,1024]{1,0:T(8,128)(2,1)} %param.13) | copy-start | bytes 6291460
  13.1 3.2 %copy-start.3 = (bf16[128,1024]{1,0:T(8,128)(2,1)S(1)}, bf16[128,1024]{1,0:T(8,128)(2,1)}, u32[]{:S(2)}) copy-start(bf16[128,1024]{1,0:T(8,128)(2,1)} %param.11) | copy-start | bytes 786436
  13.3 19.6 %copy-start.11 = (u32[128]{0:T(128)S(1)}, u32[128]{0:T(128)}, u32[]{:S(2)}) copy-start(u32[128]{0:T(128)} %constant.36) | copy-start | bytes 1540
  13.3 34.8 %copy-start.10 = (u32[128]{0:T(128)S(1)}, u32[128]{0:T(128)}, u32[]{:S(2)}) copy-start(u32[128]{0:T(128)} %constant.41) | copy-start | bytes 1540
  13.3 49.1 %copy-start.9 = (u32[128]{0:T(128)S(1)}, u32[128]{0:T(128)}, u32[]{:S(2)}) copy-start(u32[128]{0:T(128)} %constant.46) | copy-start | bytes 1540
  78.2 6.0 %copy-start.5 = (bf16[1024,128]{0,1:T(8,128)(2,1)S(1)}, bf16[1024,128]{0,1:T(8,128)(2,1)}, u32[]{:S(2)}) copy-start(bf16[1024,128]{0,1:T(8,128)(2,1)} %get-tuple-element.38) | copy-start | bytes 786436
  84.2 6.1 %slice-start = ((s8[8388608]{0:T(1024)(128)(4,1)}), s8[4194304]{0:T(1024)(128)(4,1)S(1)}, s32[]{:S(2)}) async-start(s8[8388608]{0:T(1024)(128)(4,1)} %bitcast.50), calls=%async_computation.1 | async-start | bytes 8388608
  85.6 4.9 %slice-start.1 = ((s8[8388608]{0:T(1024)(128)(4,1)}), s8[4194304]{0:T(1024)(128)(4,1)S(1)}, s32[]{:S(2)}) async-start(s8[8388608]{0:T(1024)(128)(4,1)} %bitcast.50), calls=%async_computation.2 | async-start | bytes 8388608
  90.5 1.9 copy-start.7
  115.5 15.8 %copy-start.4 = (bf16[128,1024]{1,0:T(8,128)(2,1)S(1)}, bf16[128,1024]{1,0:T(8,128)(2,1)}, u32[]{:S(2)}) copy-start(bf16[128,1024]{1,0:T(8,128)(2,1)} %param.11) | copy-start | bytes 786436
  115.5 15.7 %copy-start.6 = (bf16[1024,128]{0,1:T(8,128)(2,1)S(1)}, bf16[1024,128]{0,1:T(8,128)(2,1)}, u32[]{:S(2)}) copy-start(bf16[1024,128]{0,1:T(8,128)(2,1)} %get-tuple-element.38) | copy-start | bytes 786436
Sparse Core Ops, SparseCore 0:
  92.5 147.1 all-reduce.18
